TPU v7x, 32 devices: a whole 2x2x4 slice. The times are simulated.
32 devices in a mesh: pq: 2 (over x), rs: 16 (over z, y, core).
Axes of the slice: x: 2, y: 2, z: 4, core: 2. Of those that a mesh axis runs over, the one named last changes fastest.
Arguments:
- integrals: bfloat16 [128, 1152, 1152], P('pq', 'rs'), may hold values from -6 to 6
- coeff: bfloat16 [1152, 896], P('rs', 'pq'), may hold values from -0.1875 to 0.1875
Outputs:
- half_mo: bfloat16 [128, 896, 896], P('pq', 'rs')
All inputs are finite; a program needn't handle non-finite values.
Results may differ from a plain program's by a relative error of at most 0.0049.
Values may be sent and summed in bfloat16 or wider, within the bound.
A program may use at most 128 MiB of HBM per device.

v0:
```python
import jax
import jax.numpy as jnp
from jax import lax
from jax.sharding import PartitionSpec as P

NBASIS = 1152
NORB = 896


def second_half(received, panel):
    return jnp.einsum("prl,rk->plk", received, panel, preferred_element_type=jnp.float32).astype(
        jnp.bfloat16
    )


def on_device(integrals, coeff):
    pair_rows = integrals.shape[0]
    block_rows = integrals.shape[1]
    flat = integrals.reshape(pair_rows * block_rows, NBASIS)
    strip = lax.all_gather(coeff, "pq", axis=1, tiled=True)
    panel = lax.all_gather(strip, "rs", axis=0, tiled=True)
    first = jnp.dot(flat, panel, preferred_element_type=jnp.float32).astype(jnp.bfloat16)
    first = first.reshape(pair_rows, block_rows, NORB)
    return second_half(lax.all_to_all(first, "rs", split_axis=2, concat_axis=1, tiled=True), panel)


def solution(mesh):
    placed = (P("pq", "rs", None), P("rs", "pq"))
    return jax.shard_map(
        on_device, mesh=mesh, in_specs=placed, out_specs=P("pq", "rs", None), check_vma=False
    )
```

profile of v0, /device:TPU:1, one launch (start us, length us, event | category | flops | bytes accessed | tf_op | source)
XLA Modules:
  0.0 468.6 jit_solution(1243256376461925950)
XLA Ops:
  6.5 0.0 all-gather.3.cloned.1.call-start
  6.5 4.7 %all-gather = bf16[2,448,72]{1,2,0:T(8,128)(2,1)S(1)} all-gather(bf16[1,448,72]{1,2,0:T(8,128)(2,1)} %bitcast.25), channel_id=1, replica_groups=mesh['pq'=2,'rs'=16] {'pq'}, dimensions={0}, use_global_device_ids=true | all-gather | bytes 193536 | tf_op jit(solution)/shard_map/all_gather | solution.py:20
  11.2 0.1 copy.7
  11.3 0.8 reshape.9
  12.1 0.0 all-gather.3.cloned.1.call-update
  12.2 44.5 %all-gather.3.cloned.1.call-done = bf16[1152,896]{1,0:T(8,128)(2,1)} async-done(((bf16[72,896]{1,0:T(8,128)(2,1)}), bf16[1152,896]{1,0:T(8,128)(2,1)}) %all-gather.3.cloned.1.call-update) | async-done | bytes 2064400 | tf_op jit(solution)/shard_map/all_gather | solution.py:21
  56.7 17.5 %convolution_convert_fusion = bf16[4608,896]{1,0:T(8,128)(2,1)} fusion(bf16[4608,1152]{1,0:T(8,128)(2,1)} %bitcast.26, bf16[1152,896]{1,0:T(8,128)(2,1)} %all-gather.3.cloned.1.call-done), kind=kOutput, calls=%fused_computation | convolution fusion | flops 9516810240 | bytes 20938752 | tf_op jit(solution)/shard_map/dot_general | solution.py:22
  74.2 18.5 %copy.8 = bf16[64,72,896]{1,0,2:T(8,128)(2,1)} copy(bf16[64,72,896]{2,1,0:T(8,128)(2,1)} %bitcast.23) | data formatting | bytes 16515072 | tf_op jit(solution)/shard_map/reshape | solution.py:23
  92.7 321.5 %all_to_all.18 = bf16[64,72,896]{1,0,2:T(8,128)(2,1)S(1)} all-to-all(bf16[64,72,896]{1,0,2:T(8,128)(2,1)} %copy.8), channel_id=1, replica_groups=mesh['pq'=2,'rs'=16] {'rs'}, dimensions={2} | all-to-all | bytes 16515072 | tf_op jit(solution)/shard_map/all_to_all | solution.py:24
  414.1 10.6 %copy.10 = bf16[64,16,72,56]{2,1,3,0:T(8,128)(2,1)} copy(bf16[64,16,72,56]{2,0,3,1:T(8,128)(2,1)S(1)} %bitcast.22) | data formatting | bytes 16515072 | tf_op jit(solution)/shard_map/all_to_all | solution.py:24
  424.7 0.0 copy-start
  424.7 23.2 %all_to_all.16 = bf16[64,1152,56]{1,2,0:T(8,128)(2,1)} reshape(bf16[64,16,72,56]{2,1,3,0:T(8,128)(2,1)} %copy.10) | data formatting | bytes 16515072 | tf_op jit(solution)/shard_map/all_to_all | solution.py:24
  447.9 0.0 copy-done
  447.9 13.8 %convolution_convert_fusion.1 = bf16[64,56,896]{2,1,0:T(8,128)(2,1)} fusion(bf16[64,1152,56]{1,2,0:T(8,128)(2,1)} %all_to_all.16, bf16[1152,896]{1,0:T(8,128)(2,1)S(1)} %copy-done), kind=kOutput, calls=%fused_computation.1 | convolution fusion | flops 7401963520 | bytes 16744448 | tf_op jit(solution)/shard_map/prl,rk->plk/dot_general | solution.py:11
Async XLA Ops:
  6.5 50.2 %all-gather.3.cloned.1.call-start = ((), (), s32[]{:S(2)}) async-start(), calls=%async_computation.1 | async-start | bytes 2193408 | tf_op jit(solution)/shard_map/all_gather | solution.py:21
  424.7 23.2 %copy-start = (bf16[1152,896]{1,0:T(8,128)(2,1)S(1)}, bf16[1152,896]{1,0:T(8,128)(2,1)}, u32[]{:S(2)}) copy-start(bf16[1152,896]{1,0:T(8,128)(2,1)} %all-gather.3.cloned.1.call-done) | copy-start | bytes 6193156
Sparse Core Ops, SparseCore 0:
  12.3 44.3 all-gather.2
where the time goes:
time: 470 us; the launch traced here: 469 us
  blocking collectives  326 us (69%)
  local copies, waits for them, and re-layouts  53.2 us (11%)
  waiting for transfers between devices  44.6 us (9%)
  matrix products  31.3 us (7%)
  between operations  13.4 us (3%)
    all_to_all x1, blocking collectives, on_device(): lax.all_to_all(first, 'rs', split_axis=2, concat_axis=1, tiled=True)  321 us
    all_gather x1, waiting for transfers between devices, on_device(): panel = lax.all_gather(strip, 'rs', axis=0, tiled=True)  44.5 us
    all_to_all x2, local copies, waits for them, and re-layouts, on_device(): lax.all_to_all(first, 'rs', split_axis=2, concat_axis=1, tiled=True)  33.8 us
    reshape x1, local copies, waits for them, and re-layouts, on_device(): first = first.reshape(pair_rows, block_rows, NORB)  18.5 us
    dot_general x1, matrix products, on_device(): jnp.dot(flat, panel, preferred_element_type=jnp.float32)  17.5 us
    dot_general x1, matrix products, second_half(): jnp.einsum('prl,rk->plk', received, panel, preferred_element_type=jnp.flo...  13.8 us
  transfers between devices with their start and end apart: 1, of which 1 were waited for; matrix products, arithmetic and copies ran while one was open for 0% of the time, Pallas kernels for 0%

commit v1 on v0

--- a/solution.py
+++ b/solution.py
@@ -5,6 +5,16 @@
 
 NBASIS = 1152
 NORB = 896
+
+
+def pass_along(x, name, dim):
+    size = lax.axis_size(name)
+    held, tiles = (x, [x])
+    for _ in range(size - 1):
+        held = lax.ppermute(held, name, [(i, (i + 1) % size) for i in range(size)])
+        tiles.insert(0, held)
+    merged = jnp.concatenate(tiles, axis=dim)
+    return jnp.roll(merged, (lax.axis_index(name) + 1) * x.shape[dim], axis=dim)
 
 
 def second_half(received, panel):
@@ -18,7 +28,7 @@
     block_rows = integrals.shape[1]
     flat = integrals.reshape(pair_rows * block_rows, NBASIS)
     strip = lax.all_gather(coeff, "pq", axis=1, tiled=True)
-    panel = lax.all_gather(strip, "rs", axis=0, tiled=True)
+    panel = pass_along(strip, "rs", 0)
     first = jnp.dot(flat, panel, preferred_element_type=jnp.float32).astype(jnp.bfloat16)
     first = first.reshape(pair_rows, block_rows, NORB)
     return second_half(lax.all_to_all(first, "rs", split_axis=2, concat_axis=1, tiled=True), panel)

time: 470 us -> 532 us (1.13)
  waiting for transfers between devices: 44.6 us -> 93.3 us
  local copies, waits for them, and re-layouts: 53.2 us -> 66.4 us
  between operations: 13.4 us -> 0.22 us
  starting transfers between devices: 0.01 us -> 8.11 us
  blocking collectives: 326 us -> 332 us
    ppermute x0 -> x15, waiting for transfers between devices: none -> 93.3 us  [pass_along(): held = lax.ppermute(held, name, [(i, (i + 1) % size) for i in range(size)])]
    all_gather x1 -> x0, waiting for transfers between devices: 44.5 us -> none  [on_device(): panel = lax.all_gather(strip, 'rs', axis=0, tiled=True)]
    convert_element_type x0 -> x1, local copies, waits for them, and re-layouts: none -> 11.5 us  [on_device(): jnp.dot(flat, panel, preferred_element_type=jnp.float32)]
    ppermute x0 -> x15, starting transfers between devices: none -> 8.11 us  [pass_along(): held = lax.ppermute(held, name, [(i, (i + 1) % size) for i in range(size)])]
    all_to_all x1, blocking collectives: 321 us -> 327 us  [on_device(): lax.all_to_all(first, 'rs', split_axis=2, concat_axis=1, tiled=True)]
  transfers between devices with their start and end apart: 1 -> 15, of which waited for: 1 -> 15; matrix products, arithmetic and copies ran while one was open for 0% -> 0% of each run, Pallas kernels for 0% -> 0%
where the time goes in v1:
time: 532 us; the launch traced here: 530 us
  blocking collectives  332 us (62%)
  waiting for transfers between devices  93.3 us (18%)
  local copies, waits for them, and re-layouts  66.4 us (12%)
  matrix products  30.2 us (6%)
  starting transfers between devices  8.11 us (2%)
    all_to_all x1, blocking collectives, on_device(): lax.all_to_all(first, 'rs', split_axis=2, concat_axis=1, tiled=True)  327 us
    ppermute x15, waiting for transfers between devices, pass_along(): held = lax.ppermute(held, name, [(i, (i + 1) % size) for i in range(size)])  93.3 us
    all_to_all x2, local copies, waits for them, and re-layouts, on_device(): lax.all_to_all(first, 'rs', split_axis=2, concat_axis=1, tiled=True)  33.6 us
    reshape x1, local copies, waits for them, and re-layouts, on_device(): first = first.reshape(pair_rows, block_rows, NORB)  18.5 us
    dot_general x1, matrix products, on_device(): jnp.dot(flat, panel, preferred_element_type=jnp.float32)  15.6 us
    dot_general x1, matrix products, second_half(): jnp.einsum('prl,rk->plk', received, panel, preferred_element_type=jnp.flo...  14.5 us
    convert_element_type x1, local copies, waits for them, and re-layouts, on_device(): jnp.dot(flat, panel, preferred_element_type=jnp.float32)  11.5 us
  transfers between devices with their start and end apart: 15, of which 15 were waited for; matrix products, arithmetic and copies ran while one was open for 0% of the time, Pallas kernels for 0%

profile of v1, /device:TPU:1, one launch (start us, length us, event | category | flops | bytes accessed | tf_op | source)
XLA Modules:
  0.0 530.3 jit_solution(15003028117703383906)
XLA Ops:
  0.0 4.7 all-gather
  4.7 0.1 copy.11
  4.8 0.1 reshape.9
  5.0 3.2 collective-permute-start
  8.2 1.9 collective-permute-done
  10.1 2.4 collective-permute-start.1
  12.5 1.9 collective-permute-done.1
  14.5 2.4 collective-permute-start.2
  16.9 4.6 collective-permute-done.2
  21.5 0.0 collective-permute-start.3
  21.5 7.1 %collective-permute-done.3 = bf16[72,896]{1,0:T(8,128)(2,1)S(1)} collective-permute-done((bf16[72,896]{1,0:T(8,128)(2,1)S(1)}, bf16[72,896]{1,0:T(8,128)(2,1)S(1)}, u32[]{:S(2)}, u32[]{:S(2)}) %collective-permute-start.3) | collective-permute-done | bytes 129056 | tf_op jit(solution)/shard_map/ppermute | solution.py:14
  28.6 0.0 collective-permute-start.4
  28.6 7.1 %collective-permute-done.4 = bf16[72,896]{1,0:T(8,128)(2,1)S(1)} collective-permute-done((bf16[72,896]{1,0:T(8,128)(2,1)S(1)}, bf16[72,896]{1,0:T(8,128)(2,1)S(1)}, u32[]{:S(2)}, u32[]{:S(2)}) %collective-permute-start.4) | collective-permute-done | bytes 129056 | tf_op jit(solution)/shard_map/ppermute | solution.py:14
  35.7 0.0 collective-permute-start.5
  35.7 7.1 %collective-permute-done.5 = bf16[72,896]{1,0:T(8,128)(2,1)S(1)} collective-permute-done((bf16[72,896]{1,0:T(8,128)(2,1)S(1)}, bf16[72,896]{1,0:T(8,128)(2,1)S(1)}, u32[]{:S(2)}, u32[]{:S(2)}) %collective-permute-start.5) | collective-permute-done | bytes 129056 | tf_op jit(solution)/shard_map/ppermute | solution.py:14
  42.7 0.0 collective-permute-start.6
  42.7 7.1 %collective-permute-done.6 = bf16[72,896]{1,0:T(8,128)(2,1)S(1)} collective-permute-done((bf16[72,896]{1,0:T(8,128)(2,1)S(1)}, bf16[72,896]{1,0:T(8,128)(2,1)S(1)}, u32[]{:S(2)}, u32[]{:S(2)}) %collective-permute-start.6) | collective-permute-done | bytes 129056 | tf_op jit(solution)/shard_map/ppermute | solution.py:14
  49.8 0.0 collective-permute-start.7
  49.8 7.1 %collective-permute-done.7 = bf16[72,896]{1,0:T(8,128)(2,1)S(1)} collective-permute-done((bf16[72,896]{1,0:T(8,128)(2,1)S(1)}, bf16[72,896]{1,0:T(8,128)(2,1)S(1)}, u32[]{:S(2)}, u32[]{:S(2)}) %collective-permute-start.7) | collective-permute-done | bytes 129056 | tf_op jit(solution)/shard_map/ppermute | solution.py:14
  56.9 0.0 collective-permute-start.8
  56.9 7.1 %collective-permute-done.8 = bf16[72,896]{1,0:T(8,128)(2,1)S(1)} collective-permute-done((bf16[72,896]{1,0:T(8,128)(2,1)S(1)}, bf16[72,896]{1,0:T(8,128)(2,1)S(1)}, u32[]{:S(2)}, u32[]{:S(2)}) %collective-permute-start.8) | collective-permute-done | bytes 129056 | tf_op jit(solution)/shard_map/ppermute | solution.py:14
  63.9 0.0 collective-permute-start.9
  63.9 7.1 %collective-permute-done.9 = bf16[72,896]{1,0:T(8,128)(2,1)S(1)} collective-permute-done((bf16[72,896]{1,0:T(8,128)(2,1)S(1)}, bf16[72,896]{1,0:T(8,128)(2,1)S(1)}, u32[]{:S(2)}, u32[]{:S(2)}) %collective-permute-start.9) | collective-permute-done | bytes 129056 | tf_op jit(solution)/shard_map/ppermute | solution.py:14
  71.0 0.0 collective-permute-start.10
  71.0 7.1 %collective-permute-done.10 = bf16[72,896]{1,0:T(8,128)(2,1)S(1)} collective-permute-done((bf16[72,896]{1,0:T(8,128)(2,1)S(1)}, bf16[72,896]{1,0:T(8,128)(2,1)S(1)}, u32[]{:S(2)}, u32[]{:S(2)}) %collective-permute-start.10) | collective-permute-done | bytes 129056 | tf_op jit(solution)/shard_map/ppermute | solution.py:14
  78.1 0.0 collective-permute-start.11
  78.1 7.1 %collective-permute-done.11 = bf16[72,896]{1,0:T(8,128)(2,1)S(1)} collective-permute-done((bf16[72,896]{1,0:T(8,128)(2,1)S(1)}, bf16[72,896]{1,0:T(8,128)(2,1)S(1)}, u32[]{:S(2)}, u32[]{:S(2)}) %collective-permute-start.11) | collective-permute-done | bytes 129056 | tf_op jit(solution)/shard_map/ppermute | solution.py:14
  85.1 0.0 collective-permute-start.12
  85.1 7.1 %collective-permute-done.12 = bf16[72,896]{1,0:T(8,128)(2,1)S(1)} collective-permute-done((bf16[72,896]{1,0:T(8,128)(2,1)S(1)}, bf16[72,896]{1,0:T(8,128)(2,1)S(1)}, u32[]{:S(2)}, u32[]{:S(2)}) %collective-permute-start.12) | collective-permute-done | bytes 129056 | tf_op jit(solution)/shard_map/ppermute | solution.py:14
  92.2 0.0 collective-permute-start.13
  92.2 7.1 %collective-permute-done.13 = bf16[72,896]{1,0:T(8,128)(2,1)S(1)} collective-permute-done((bf16[72,896]{1,0:T(8,128)(2,1)S(1)}, bf16[72,896]{1,0:T(8,128)(2,1)S(1)}, u32[]{:S(2)}, u32[]{:S(2)}) %collective-permute-start.13) | collective-permute-done | bytes 129056 | tf_op jit(solution)/shard_map/ppermute | solution.py:14
  99.3 0.0 collective-permute-start.14
  99.3 7.1 %collective-permute-done.14 = bf16[72,896]{1,0:T(8,128)(2,1)S(1)} collective-permute-done((bf16[72,896]{1,0:T(8,128)(2,1)S(1)}, bf16[72,896]{1,0:T(8,128)(2,1)S(1)}, u32[]{:S(2)}, u32[]{:S(2)}) %collective-permute-start.14) | collective-permute-done | bytes 129056 | tf_op jit(solution)/shard_map/ppermute | solution.py:14
  107.1 0.0 copy-start
  107.1 2.0 copy-done
  109.1 15.6 %fusion = bf16[4608,896]{0,1:T(8,128)(2,1)} fusion(bf16[4608,1152]{1,0:T(8,128)(2,1)} %bitcast.29, bf16[2304,896]{1,0:T(8,128)(2,1)S(1)} %constant_dynamic-update-slice_fusion, s32[]{:T(128)S(6)} %select_n.14), kind=kOutput, calls=%fused_computation.1 | convolution fusion | flops 9516810240 | bytes 20938756 | tf_op jit(solution)/shard_map/dot_general | solution.py:32
  124.8 11.5 %copy.12 = bf16[4608,896]{1,0:T(8,128)(2,1)} copy(bf16[4608,896]{0,1:T(8,128)(2,1)} %fusion) | data formatting | bytes 16515072 | tf_op jit(solution)/shard_map/convert_element_type | solution.py:32
  136.3 18.5 %copy.13 = bf16[64,72,896]{1,0,2:T(8,128)(2,1)} copy(bf16[64,72,896]{2,1,0:T(8,128)(2,1)} %bitcast.26) | data formatting | bytes 16515072 | tf_op jit(solution)/shard_map/reshape | solution.py:33
  154.8 327.4 %all_to_all.18 = bf16[64,72,896]{1,0,2:T(8,128)(2,1)S(1)} all-to-all(bf16[64,72,896]{1,0,2:T(8,128)(2,1)} %copy.13), channel_id=1, replica_groups=mesh['pq'=2,'rs'=16] {'rs'}, dimensions={2} | all-to-all | bytes 16515072 | tf_op jit(solution)/shard_map/all_to_all | solution.py:34
  482.2 10.5 %copy.15 = bf16[64,16,72,56]{2,1,3,0:T(8,128)(2,1)} copy(bf16[64,16,72,56]{2,0,3,1:T(8,128)(2,1)S(1)} %bitcast.25) | data formatting | bytes 16515072 | tf_op jit(solution)/shard_map/all_to_all | solution.py:34
  492.7 23.1 %all_to_all.16 = bf16[64,1152,56]{1,2,0:T(8,128)(2,1)} reshape(bf16[64,16,72,56]{2,1,3,0:T(8,128)(2,1)} %copy.15) | data formatting | bytes 16515072 | tf_op jit(solution)/shard_map/all_to_all | solution.py:34
  515.7 14.5 %convolution_convert_fusion.1 = bf16[64,56,896]{2,1,0:T(8,128)(2,1)} fusion(bf16[64,1152,56]{1,2,0:T(8,128)(2,1)} %all_to_all.16, bf16[2304,896]{1,0:T(8,128)(2,1)} %copy-done, s32[]{:T(128)S(6)} %select_n.14), kind=kOutput, calls=%fused_computation.2 | convolution fusion | flops 7401963520 | bytes 16744452 | tf_op jit(solution)/shard_map/prl,rk->plk/dot_general | solution.py:21
  (32 shorter events, 0.6 us)
Async XLA Ops:
  5.0 5.1 collective-permute-start
  10.1 4.4 collective-permute-start.1
  14.5 7.1 %collective-permute-start.2 = (bf16[72,896]{1,0:T(8,128)(2,1)S(1)}, bf16[72,896]{1,0:T(8,128)(2,1)S(1)}, u32[]{:S(2)}, u32[]{:S(2)}) collective-permute-start(bf16[72,896]{1,0:T(8,128)(2,1)S(1)} %collective-permute-done.1), channel_id=1, source_target_pairs={{0,1},{1,2},{2,3},{3,4},{4,5},{5,6},{6,7},{7,8},{8,9},{9,10},{10,1... | collective-permute-start | bytes 387080 | tf_op jit(solution)/shard_map/ppermute | solution.py:14
  21.5 7.1 %collective-permute-start.3 = (bf16[72,896]{1,0:T(8,128)(2,1)S(1)}, bf16[72,896]{1,0:T(8,128)(2,1)S(1)}, u32[]{:S(2)}, u32[]{:S(2)}) collective-permute-start(bf16[72,896]{1,0:T(8,128)(2,1)S(1)} %collective-permute-done.2), channel_id=1, source_target_pairs={{0,1},{1,2},{2,3},{3,4},{4,5},{5,6},{6,7},{7,8},{8,9},{9,10},{10,1... | collective-permute-start | bytes 387080 | tf_op jit(solution)/shard_map/ppermute | solution.py:14
  28.6 7.1 %collective-permute-start.4 = (bf16[72,896]{1,0:T(8,128)(2,1)S(1)}, bf16[72,896]{1,0:T(8,128)(2,1)S(1)}, u32[]{:S(2)}, u32[]{:S(2)}) collective-permute-start(bf16[72,896]{1,0:T(8,128)(2,1)S(1)} %collective-permute-done.3), channel_id=1, source_target_pairs={{0,1},{1,2},{2,3},{3,4},{4,5},{5,6},{6,7},{7,8},{8,9},{9,10},{10,1... | collective-permute-start | bytes 387080 | tf_op jit(solution)/shard_map/ppermute | solution.py:14
  35.7 7.1 %collective-permute-start.5 = (bf16[72,896]{1,0:T(8,128)(2,1)S(1)}, bf16[72,896]{1,0:T(8,128)(2,1)S(1)}, u32[]{:S(2)}, u32[]{:S(2)}) collective-permute-start(bf16[72,896]{1,0:T(8,128)(2,1)S(1)} %collective-permute-done.4), channel_id=1, source_target_pairs={{0,1},{1,2},{2,3},{3,4},{4,5},{5,6},{6,7},{7,8},{8,9},{9,10},{10,1... | collective-permute-start | bytes 387080 | tf_op jit(solution)/shard_map/ppermute | solution.py:14
  42.7 7.1 %collective-permute-start.6 = (bf16[72,896]{1,0:T(8,128)(2,1)S(1)}, bf16[72,896]{1,0:T(8,128)(2,1)S(1)}, u32[]{:S(2)}, u32[]{:S(2)}) collective-permute-start(bf16[72,896]{1,0:T(8,128)(2,1)S(1)} %collective-permute-done.5), channel_id=1, source_target_pairs={{0,1},{1,2},{2,3},{3,4},{4,5},{5,6},{6,7},{7,8},{8,9},{9,10},{10,1... | collective-permute-start | bytes 387080 | tf_op jit(solution)/shard_map/ppermute | solution.py:14
  49.8 7.1 %collective-permute-start.7 = (bf16[72,896]{1,0:T(8,128)(2,1)S(1)}, bf16[72,896]{1,0:T(8,128)(2,1)S(1)}, u32[]{:S(2)}, u32[]{:S(2)}) collective-permute-start(bf16[72,896]{1,0:T(8,128)(2,1)S(1)} %collective-permute-done.6), channel_id=1, source_target_pairs={{0,1},{1,2},{2,3},{3,4},{4,5},{5,6},{6,7},{7,8},{8,9},{9,10},{10,1... | collective-permute-start | bytes 387080 | tf_op jit(solution)/shard_map/ppermute | solution.py:14
  56.9 7.1 %collective-permute-start.8 = (bf16[72,896]{1,0:T(8,128)(2,1)S(1)}, bf16[72,896]{1,0:T(8,128)(2,1)S(1)}, u32[]{:S(2)}, u32[]{:S(2)}) collective-permute-start(bf16[72,896]{1,0:T(8,128)(2,1)S(1)} %collective-permute-done.7), channel_id=1, source_target_pairs={{0,1},{1,2},{2,3},{3,4},{4,5},{5,6},{6,7},{7,8},{8,9},{9,10},{10,1... | collective-permute-start | bytes 387080 | tf_op jit(solution)/shard_map/ppermute | solution.py:14
  63.9 7.1 %collective-permute-start.9 = (bf16[72,896]{1,0:T(8,128)(2,1)S(1)}, bf16[72,896]{1,0:T(8,128)(2,1)S(1)}, u32[]{:S(2)}, u32[]{:S(2)}) collective-permute-start(bf16[72,896]{1,0:T(8,128)(2,1)S(1)} %collective-permute-done.8), channel_id=1, source_target_pairs={{0,1},{1,2},{2,3},{3,4},{4,5},{5,6},{6,7},{7,8},{8,9},{9,10},{10,1... | collective-permute-start | bytes 387080 | tf_op jit(solution)/shard_map/ppermute | solution.py:14
  71.0 7.1 %collective-permute-start.10 = (bf16[72,896]{1,0:T(8,128)(2,1)S(1)}, bf16[72,896]{1,0:T(8,128)(2,1)S(1)}, u32[]{:S(2)}, u32[]{:S(2)}) collective-permute-start(bf16[72,896]{1,0:T(8,128)(2,1)S(1)} %collective-permute-done.9), channel_id=1, source_target_pairs={{0,1},{1,2},{2,3},{3,4},{4,5},{5,6},{6,7},{7,8},{8,9},{9,10},{10,1... | collective-permute-start | bytes 387080 | tf_op jit(solution)/shard_map/ppermute | solution.py:14
  78.1 7.1 %collective-permute-start.11 = (bf16[72,896]{1,0:T(8,128)(2,1)S(1)}, bf16[72,896]{1,0:T(8,128)(2,1)S(1)}, u32[]{:S(2)}, u32[]{:S(2)}) collective-permute-start(bf16[72,896]{1,0:T(8,128)(2,1)S(1)} %collective-permute-done.10), channel_id=1, source_target_pairs={{0,1},{1,2},{2,3},{3,4},{4,5},{5,6},{6,7},{7,8},{8,9},{9,10},{10,1... | collective-permute-start | bytes 387080 | tf_op jit(solution)/shard_map/ppermute | solution.py:14
  85.1 7.1 %collective-permute-start.12 = (bf16[72,896]{1,0:T(8,128)(2,1)S(1)}, bf16[72,896]{1,0:T(8,128)(2,1)S(1)}, u32[]{:S(2)}, u32[]{:S(2)}) collective-permute-start(bf16[72,896]{1,0:T(8,128)(2,1)S(1)} %collective-permute-done.11), channel_id=1, source_target_pairs={{0,1},{1,2},{2,3},{3,4},{4,5},{5,6},{6,7},{7,8},{8,9},{9,10},{10,1... | collective-permute-start | bytes 387080 | tf_op jit(solution)/shard_map/ppermute | solution.py:14
  92.2 7.1 %collective-permute-start.13 = (bf16[72,896]{1,0:T(8,128)(2,1)S(1)}, bf16[72,896]{1,0:T(8,128)(2,1)S(1)}, u32[]{:S(2)}, u32[]{:S(2)}) collective-permute-start(bf16[72,896]{1,0:T(8,128)(2,1)S(1)} %collective-permute-done.12), channel_id=1, source_target_pairs={{0,1},{1,2},{2,3},{3,4},{4,5},{5,6},{6,7},{7,8},{8,9},{9,10},{10,1... | collective-permute-start | bytes 387080 | tf_op jit(solution)/shard_map/ppermute | solution.py:14
  99.3 7.1 %collective-permute-start.14 = (bf16[72,896]{1,0:T(8,128)(2,1)S(1)}, bf16[72,896]{1,0:T(8,128)(2,1)S(1)}, u32[]{:S(2)}, u32[]{:S(2)}) collective-permute-start(bf16[72,896]{1,0:T(8,128)(2,1)S(1)} %collective-permute-done.13), channel_id=1, source_target_pairs={{0,1},{1,2},{2,3},{3,4},{4,5},{5,6},{6,7},{7,8},{8,9},{9,10},{10,1... | collective-permute-start | bytes 387080 | tf_op jit(solution)/shard_map/ppermute | solution.py:14
  107.1 2.0 copy-start
